TPU v7x, 32 devices: a whole 2x2x4 slice. The times are simulated.
32 devices in a mesh: gz: 8 (over z, x), rows: 4 (over y, core).
Axes of the slice: x: 2, y: 2, z: 4, core: 2. Of those that a mesh axis runs over, the one named last changes fastest.
Arguments:
- sections: bfloat16 [8, 1024, 4096], P('gz', 'rows'), may hold values from -4 to 4
- peaks: int32 [8, 2, 1, 4], P('gz'), may hold values from -16 to 16, as said below
Outputs:
- field: float32 [8, 2, 1024, 4096], P('gz', None, 'rows')
- pair_offsets: float32 [8, 2, 1, 4], P('gz')
- residual: bfloat16 [8, 1024, 4096], P('gz', 'rows')
Inputs may be any that keep to these rules, and one draw needn't show every extreme that they name: `peaks`: in every draw the first section's first patch has row offset 16 and column offset -16.
All inputs are finite; a program needn't handle non-finite values.
Results may differ from a plain program's by a relative error of at most 0.001.
Values may be sent and summed in bfloat16 or wider, within the bound.
A program may use at most 64 MiB of HBM per device.

v0:
```python
import jax
import jax.numpy as jnp
import numpy as np
from jax import lax
from jax.sharding import PartitionSpec as P

PATCH = 1024
MAXOFF = 16


LAMBDA = 0.002
RIDGE = 0.05


def from_behind(value, axis, steps):
    count = lax.axis_size(axis)
    first, last = (max(0, -steps), min(count, count - steps))
    return lax.ppermute(value, axis, [(source, source + steps) for source in range(first, last)])


def with_halo(cells, sides, width):
    for axis, dim in sides:
        count = lax.axis_size(axis)
        ends = count - 1
        head = lax.slice_in_dim(cells, 0, width, axis=dim)
        tail = lax.slice_in_dim(cells, cells.shape[dim] - width, cells.shape[dim], axis=dim)
        cells = jnp.concatenate(
            [
                lax.ppermute(tail, axis, [(i, (i + 1) % count) for i in range(ends)]),
                cells,
                lax.ppermute(head, axis, [((i + 1) % count, i) for i in range(ends)]),
            ],
            axis=dim,
        )
    return cells


def entering(value, axis, combine, identity):
    length, here = (lax.axis_size(axis), lax.axis_index(axis))
    everything = jax.tree.map(lambda part: lax.all_gather(part, axis), value)
    start = jax.tree.map(
        lambda part, zero: jnp.broadcast_to(jnp.asarray(zero, part.dtype), part.shape),
        value,
        identity,
    )

    def step(k, before):
        reached = k < here
        new = combine(before, jax.tree.map(lambda part: part[k], everything))
        return jax.tree.map(lambda a, b: jnp.where(reached, a, b), new, before)

    return lax.fori_loop(0, length, step, start)


def invert_three(matrix):
    a, b, c = (matrix[0, 0], matrix[0, 1], matrix[0, 2])
    d, e, f = (matrix[1, 0], matrix[1, 1], matrix[1, 2])
    g, h, k = (matrix[2, 0], matrix[2, 1], matrix[2, 2])
    cof = np.array(
        [
            [e * k - f * h, c * h - b * k, b * f - c * e],
            [f * g - d * k, a * k - c * g, c * d - a * f],
            [d * h - e * g, b * g - a * h, a * e - b * d],
        ]
    )
    return cof / (a * (e * k - f * h) - b * (d * k - f * g) + c * (d * h - e * g))


def fit_table(pgy, pgx, patch, height, width):
    yy = ((np.arange(pgy) + 0.5) * patch - height / 2.0) / height
    xx = ((np.arange(pgx) + 0.5) * patch - width / 2.0) / width
    design = np.stack([np.repeat(yy, pgx), np.tile(xx, pgy), np.ones(pgy * pgx)], 1)
    ridge_matrix = np.array([[RIDGE, 0.0, 0.0], [0.0, RIDGE, 0.0], [0.0, 0.0, 0.0]])
    gram = design.T @ design + ridge_matrix
    return invert_three(gram) @ design.T


def spread(count, patch, nodes, start):
    pos = (start + jnp.arange(count).astype(jnp.float32) + 0.5) / patch - 0.5
    pos = jnp.clip(pos, 0.0, nodes - 1.0)
    return jnp.maximum(
        0.0, 1.0 - jnp.abs(pos[:, None] - jnp.arange(nodes).astype(jnp.float32)[None, :])
    )


def moments(current, window):
    centre = window[1:-1, 1:-1]
    grad_y = (window[2:, 1:-1] - window[:-2, 1:-1]) * 0.5
    grad_x = (window[1:-1, 2:] - window[1:-1, :-2]) * 0.5
    error = current - centre
    sums = jnp.stack(
        [
            jnp.sum(grad_y * grad_y),
            jnp.sum(grad_y * grad_x),
            jnp.sum(grad_x * grad_x),
            jnp.sum(grad_y * error),
            jnp.sum(grad_x * error),
        ]
    )
    return (sums, error)


def solve_pairs(sums, peak_grid):
    damping = LAMBDA * PATCH * PATCH
    first = sums[0] + damping
    cross = sums[1]
    second = sums[2] + damping
    determinant = first * second - cross * cross
    step_y = (second * sums[3] - cross * sums[4]) / determinant
    step_x = (first * sums[4] - cross * sums[3]) / determinant
    return peak_grid.astype(jnp.float32) + jnp.stack([step_y, step_x])


def transform(offsets, table, height, width):
    flat = offsets.reshape(2, -1)
    coef = jnp.dot(flat, table.T, precision=lax.Precision.HIGHEST)
    return jnp.eye(2, dtype=jnp.float32) + jnp.stack(
        [coef[:, 0] / height, coef[:, 1] / width], axis=1
    )


def compose(earlier, later):
    linear = jnp.dot(later[0], earlier[0], precision=lax.Precision.HIGHEST)
    offset = jnp.dot(later[0], earlier[1], precision=lax.Precision.HIGHEST) + later[1]
    return (linear, offset)


def per_device(sections, peaks):
    band_rows = sections.shape[1]
    width = sections.shape[2]
    height = band_rows * lax.axis_size("rows")
    pgy = height // PATCH
    pgx = width // PATCH
    margin = MAXOFF + 1
    position = lax.axis_index("rows")
    before = from_behind(sections, "gz", 1)
    extended = with_halo(before, (("rows", 1),), margin)
    padded = jnp.pad(extended[0].astype(jnp.float32), ((0, 0), (margin, margin)))
    patch_row = position * band_rows // PATCH
    local_peaks = lax.dynamic_index_in_dim(peaks[0], patch_row, axis=1, keepdims=False)
    current = sections[0].astype(jnp.float32)
    values = []
    errors = []
    for j in range(pgx):
        start_y = margin - 1 + local_peaks[0, j]
        start_x = j * PATCH + margin - 1 + local_peaks[1, j]
        window = lax.dynamic_slice(padded, (start_y, start_x), (band_rows + 2, PATCH + 2))
        sums_one, error_one = moments(current[:, j * PATCH : (j + 1) * PATCH], window)
        values.append(sums_one)
        errors.append(error_one)
    residual = jnp.concatenate(errors, axis=1).astype(jnp.bfloat16)
    stacked = jnp.stack(values, axis=1)
    select = (jnp.arange(pgy) == patch_row).astype(jnp.float32)
    placed = select[None, :, None] * stacked[:, None, :]
    sums = lax.psum(placed, "rows")
    offsets = solve_pairs(sums, peaks[0])
    table = jnp.asarray(fit_table(pgy, pgx, PATCH, height, width), jnp.float32)
    linear = transform(offsets, table, height, width)
    flat = offsets.reshape(2, -1)
    identity = (jnp.eye(2, dtype=jnp.float32), jnp.zeros_like(flat))
    prior = entering((linear, flat), "gz", compose, identity)
    nodes = jnp.dot(linear, prior[1], precision=lax.Precision.HIGHEST) + flat
    along_rows = spread(band_rows, PATCH, pgy, (position * band_rows).astype(jnp.float32))
    along_cols = spread(width, PATCH, pgx, 0)
    grid = nodes.reshape(2, pgy, pgx)
    wide = jnp.einsum("kij,cj->kic", grid, along_cols, precision=lax.Precision.HIGHEST)
    field = jnp.einsum("ri,kic->krc", along_rows, wide, precision=lax.Precision.HIGHEST)
    return (field[None], offsets[None], residual[None])


def solution(mesh):
    placed = (P("gz", "rows", None), P("gz", None, None, None))
    return jax.shard_map(
        per_device,
        mesh=mesh,
        in_specs=placed,
        out_specs=(P("gz", None, "rows", None), P("gz", None, None, None), P("gz", "rows", None)),
        check_vma=False,
    )
```

profile of v0, /device:TPU:0, one launch (start us, length us, event | category | flops | bytes accessed | tf_op | source)
XLA Modules:
  0.0 150.9 jit_solution(7182604214236039344)
XLA Ops:
  0.6 5.0 %collective-permute-start = (bf16[1,256,4096]{2,1,0:T(8,128)(2,1)}, bf16[1,256,4096]{2,1,0:T(8,128)(2,1)S(1)}, u32[]{:S(2)}, u32[]{:S(2)}) collective-permute-start(bf16[1,256,4096]{2,1,0:T(8,128)(2,1)} %param.5), channel_id=1, source_target_pairs={{0,4},{4,8},{8,12},{12,16},{16,20},{20,24},{24,28},{1,5},{5,9},{9,... | collective-permute-start | bytes 6291464 | tf_op jit(solution)/shard_map/ppermute | solution.py:18
  5.7 1.7 %fusion.41 = (s32[1,1]{1,0:T(1,128)}, s32[1,1]{1,0:T(1,128)}, s32[1,1]{1,0:T(1,128)}, s32[1,1]{1,0:T(1,128)}, s32[1,1]{1,0:T(1,128)}, /*index=5*/s32[1,1]{1,0:T(1,128)}, s32[1,1]{1,0:T(1,128)}, s32[1,1]{1,0:T(1,128)}) fusion(s32[2,4]{1,0:T(2,128)} %bitcast.78), kind=kLoop, calls=%fused_computation.99 | loop fusion | bytes 64 | tf_op jit(solution)/shard_map/slice | solution.py:146
  7.3 4.1 %bitcast_convert_fusion = f32[256,4096]{1,0:T(8,128)} fusion(bf16[1,256,4096]{2,1,0:T(8,128)(2,1)} %param.5), kind=kLoop, calls=%fused_computation.13 | loop fusion | flops 1048576 | bytes 6291456 | tf_op jit(solution)/shard_map/convert_element_type | solution.py:141
  11.4 39.3 %collective-permute-done = bf16[1,256,4096]{2,1,0:T(8,128)(2,1)S(1)} collective-permute-done((bf16[1,256,4096]{2,1,0:T(8,128)(2,1)}, bf16[1,256,4096]{2,1,0:T(8,128)(2,1)S(1)}, u32[]{:S(2)}, u32[]{:S(2)}) %collective-permute-start) | collective-permute-done | bytes 2097184 | tf_op jit(solution)/shard_map/ppermute | solution.py:18
  50.8 1.3 collective-permute-start.1
  52.1 1.3 collective-permute-start.2
  63.4 0.6 maximum_bitcast_fusion
  64.0 0.8 pad_convert_fusion
  64.8 1.4 copy-done
  66.2 5.1 %convert_bitcast_fusion.3 = (bf16[1,256,1024]{2,1,0:T(8,128)(2,1)}, f32[256,1024]{1,0:T(8,128)}, bf16[1,256,1024]{2,1,0:T(8,128)(2,1)}, f32[256,1024]{1,0:T(8,12...) fusion(f32[290,4130]{1,0:T(8,128)S(1)} %pad_convert_fusion, ...), kind=kLoop, calls=%fused_computation.58 | loop fusion | flops 3145728 | bytes 20971568 | tf_op jit(solution)/shard_map/concatenate | solution.py:151
  71.3 5.1 %fusion.15 = (f32[256,1024]{1,0:T(8,128)S(1)}, f32[256,1024]{1,0:T(8,128)S(1)}, f32[256,1024]{1,0:T(8,128)}, f32[256,1024]{1,0:T(8,128)S(1)}, f32[256,1024]{1,0:T(8,128)}, /*index=5*/f32[256,1024]{1,0:T(8,128)}) fusion(f32[290,4130]{1,0:T(8,128)S(1)} %pad_convert_fusion, s32[]{:T(128)S(6)} %select_n.54, s32[]{:T(128)S(6)} %add.254, s32[]{:T(128)S(6)} %add.253, ...), kind=kLoop, calls=%fused_computation.34 | loop fusion | flops 3145728 | bytes 18874440 | tf_op jit(solution)/shard_map/mul | solution.py:88
  76.4 2.7 %multiply_reduce_fusion.10 = (f32[]{:T(128)}, f32[]{:T(128)}, f32[]{:T(128)}, f32[]{:T(128)}, f32[]{:T(128)}, /*index=5*/f32[]{:T(128)}, f32[]{:T(128)}, f32[]{:T(128)}, f32[]{:T(128)}, f32[]{:T(128)}) fusion(f32[256,1024]{1,0:T(8,128)S(1)} %get-tuple-element.177, f32[256,1024]{1,0:T(8,128)S(1)} %copy-done.3, f32[256,1024]{1,0:T(8,128)S(1)} %get-tuple-element.179, ...), kind=kLoop, calls=%fused_computation.45 | loop fusion | flops 5242870 | bytes 6291496 | tf_op jit(solution)/shard_map/reduce_sum | solution.py:97
  79.1 3.3 %stack.120 = f32[5]{0:T(128)S(1)} concatenate(f32[1]{0:T(128)} %bitcast.6, f32[1]{0:T(128)} %bitcast.7, f32[1]{0:T(128)} %bitcast.8, f32[1]{0:T(128)} %bitcast.10, f32[1]{0:T(128)} %bitcast.11), dimensions={0} | concatenate | bytes 40 | tf_op jit(solution)/shard_map/stack | solution.py:91
  82.4 3.3 %stack.127 = f32[5]{0:T(128)S(1)} concatenate(f32[1]{0:T(128)} %bitcast.17, f32[1]{0:T(128)} %bitcast.18, f32[1]{0:T(128)} %bitcast.19, f32[1]{0:T(128)} %bitcast.21, f32[1]{0:T(128)} %bitcast.22), dimensions={0} | concatenate | bytes 40 | tf_op jit(solution)/shard_map/stack | solution.py:91
  85.7 3.2 %multiply_reduce_fusion = (f32[]{:T(128)}, f32[]{:T(128)}, f32[]{:T(128)}, f32[]{:T(128)}, f32[]{:T(128)}, /*index=5*/f32[]{:T(128)}, f32[]{:T(128)}, f32[]{:T(128)}, f32[]{:T(128)}, f32[]{:T(128)}) fusion(f32[256,1024]{1,0:T(8,128)} %get-tuple-element.183, f32[256,1024]{1,0:T(8,128)S(1)} %get-tuple-element.171, f32[256,1024]{1,0:T(8,128)} %get-tuple-element.180, ...), kind=kLoop, calls=%fused_computation.35 | loop fusion | flops 5242870 | bytes 6291496 | tf_op jit(solution)/shard_map/reduce_sum | solution.py:97
  88.9 3.2 %stack.134 = f32[5]{0:T(128)S(1)} concatenate(f32[1]{0:T(128)} %bitcast.28, f32[1]{0:T(128)} %bitcast.29, f32[1]{0:T(128)} %bitcast.30, f32[1]{0:T(128)} %bitcast.31, f32[1]{0:T(128)} %bitcast.32), dimensions={0} | concatenate | bytes 40 | tf_op jit(solution)/shard_map/stack | solution.py:91
  92.1 3.2 %stack.141 = f32[5]{0:T(128)S(1)} concatenate(f32[1]{0:T(128)} %bitcast.38, f32[1]{0:T(128)} %bitcast.39, f32[1]{0:T(128)} %bitcast.40, f32[1]{0:T(128)} %bitcast.41, f32[1]{0:T(128)} %bitcast.42), dimensions={0} | concatenate | bytes 40 | tf_op jit(solution)/shard_map/stack | solution.py:91
  95.3 8.5 %psum.7 = f32[5,1,4]{0,2,1:T(4,128)S(1)} all-reduce(f32[5,1,4]{0,2,1:T(4,128)S(1)} %maximum_multiply_fusion), channel_id=1, replica_groups=mesh['gz'=8,'rows'=4] {'rows'}, use_global_device_ids=true, to_apply=%region_20.21 | all-reduce | flops 20 | bytes 160 | tf_op jit(solution)/shard_map/psum | solution.py:155
  104.3 21.6 %all_gather.8 = f32[8,2,4]{2,1,0:T(2,128)S(1)} all-gather(f32[1,2,4]{2,1,0:T(2,128)S(1)} %maximum_add_fusion.1), channel_id=1, replica_groups=mesh['gz'=8,'rows'=4] {'gz'}, dimensions={0}, use_global_device_ids=true | all-gather | bytes 288 | tf_op jit(solution)/shard_map/all_gather | solution.py:40
  126.4 16.3 %all_gather.7 = f32[8,2,2]{2,1,0:T(2,128)S(1)} all-gather(f32[1,2,2]{2,1,0:T(2,128)S(1)} %copy.15), channel_id=1, replica_groups=mesh['gz'=8,'rows'=4] {'gz'}, dimensions={0}, use_global_device_ids=true | all-gather | bytes 144 | tf_op jit(solution)/shard_map/all_gather | solution.py:40
  142.7 1.2 while.14
  143.8 0.6 maximum_add_fusion.2
  145.0 4.4 %multiply_bitcast_fusion = f32[1,2,256,4096]{3,2,1,0:T(8,128)} fusion(f32[256]{0:T(256)S(1)} %subtract_maximum_fusion, f32[2,4096]{1,0:T(2,128)S(1)} %fusion.16), kind=kLoop, calls=%fused_computation.9 | loop fusion | flops 2097152 | bytes 8422400 | tf_op jit(solution)/shard_map/broadcast_in_dim | solution.py:168
  149.4 1.5 pad_maximum_fusion
  (55 shorter events, 2.6 us)
Async XLA Ops:
  0.6 62.7 %copy-start.8 = (s32[1,2,1,4]{3,2,1,0:T(1,128)S(1)}, s32[1,2,1,4]{3,2,1,0:T(1,128)}, u32[]{:S(2)}) copy-start(s32[1,2,1,4]{3,2,1,0:T(1,128)} %param.6) | copy-start | bytes 100
  0.6 50.1 %collective-permute-start = (bf16[1,256,4096]{2,1,0:T(8,128)(2,1)}, bf16[1,256,4096]{2,1,0:T(8,128)(2,1)S(1)}, u32[]{:S(2)}, u32[]{:S(2)}) collective-permute-start(bf16[1,256,4096]{2,1,0:T(8,128)(2,1)} %param.5), channel_id=1, source_target_pairs={{0,4},{4,8},{8,12},{12,16},{16,20},{20,24},{24,28},{1,5},{5,9},{9,... | collective-permute-start | bytes 6291464 | tf_op jit(solution)/shard_map/ppermute | solution.py:18
  50.8 12.6 %collective-permute-start.1 = (bf16[1,17,4096]{2,1,0:T(8,128)(2,1)S(1)}, bf16[1,17,4096]{2,1,0:T(8,128)(2,1)S(1)}, u32[]{:S(2)}, u32[]{:S(2)}) collective-permute-start(bf16[1,17,4096]{2,1,0:T(8,128)(2,1)S(1)} %get-tuple-element.184), channel_id=1, source_target_pairs={{0,1},{1,2},{2,3},{4,5},{5,6},{6,7},{8,9},{9,10},{10,11},{12,13},{... | collective-permute-start | bytes 417800 | tf_op jit(solution)/shard_map/ppermute | solution.py:29
  52.1 11.3 %collective-permute-start.2 = (bf16[1,17,4096]{2,1,0:T(8,128)(2,1)S(1)}, bf16[1,17,4096]{2,1,0:T(8,128)(2,1)S(1)}, u32[]{:S(2)}, u32[]{:S(2)}) collective-permute-start(bf16[1,17,4096]{2,1,0:T(8,128)(2,1)S(1)} %get-tuple-element.185), channel_id=1, source_target_pairs={{1,0},{2,1},{3,2},{5,4},{6,5},{7,6},{9,8},{10,9},{11,10},{13,12},{... | collective-permute-start | bytes 417800 | tf_op jit(solution)/shard_map/ppermute | solution.py:31
  64.0 2.2 %copy-start = (f32[256,4096]{1,0:T(8,128)S(1)}, f32[256,4096]{1,0:T(8,128)}, u32[]{:S(2)}) copy-start(f32[256,4096]{1,0:T(8,128)} %bitcast_convert_fusion) | copy-start | bytes 12582916
  71.3 5.1 %copy-start.2 = (f32[256,1024]{1,0:T(8,128)S(1)}, f32[256,1024]{1,0:T(8,128)}, u32[]{:S(2)}) copy-start(f32[256,1024]{1,0:T(8,128)} %get-tuple-element.159) | copy-start | bytes 3145732
  71.3 5.1 %copy-start.3 = (f32[256,1024]{1,0:T(8,128)S(1)}, f32[256,1024]{1,0:T(8,128)}, u32[]{:S(2)}) copy-start(f32[256,1024]{1,0:T(8,128)} %get-tuple-element.175) | copy-start | bytes 3145732
  76.4 9.3 %copy-start.1 = (f32[256,1024]{1,0:T(8,128)S(1)}, f32[256,1024]{1,0:T(8,128)}, u32[]{:S(2)}) copy-start(f32[256,1024]{1,0:T(8,128)} %get-tuple-element.182) | copy-start | bytes 3145732
  79.1 46.8 %copy-start.9 = (f32[3,4]{1,0:T(4,128)S(1)}, f32[3,4]{1,0:T(4,128)}, u32[]{:S(2)}) copy-start(f32[3,4]{1,0:T(4,128)} %constant.129.clone) | copy-start | bytes 148
  145.0 4.5 %copy-start.4 = (bf16[1,256,1024]{2,1,0:T(8,128)(2,1)S(1)}, bf16[1,256,1024]{2,1,0:T(8,128)(2,1)}, u32[]{:S(2)}) copy-start(bf16[1,256,1024]{2,1,0:T(8,128)(2,1)} %get-tuple-element.158) | copy-start | bytes 1572868
  145.0 4.5 %copy-start.5 = (bf16[1,256,1024]{2,1,0:T(8,128)(2,1)S(1)}, bf16[1,256,1024]{2,1,0:T(8,128)(2,1)}, u32[]{:S(2)}) copy-start(bf16[1,256,1024]{2,1,0:T(8,128)(2,1)} %get-tuple-element.170) | copy-start | bytes 1572868
  145.0 4.4 %copy-start.6 = (bf16[1,256,1024]{2,1,0:T(8,128)(2,1)S(1)}, bf16[1,256,1024]{2,1,0:T(8,128)(2,1)}, u32[]{:S(2)}) copy-start(bf16[1,256,1024]{2,1,0:T(8,128)(2,1)} %get-tuple-element.172) | copy-start | bytes 1572868
  145.0 4.4 %copy-start.7 = (bf16[1,256,1024]{2,1,0:T(8,128)(2,1)S(1)}, bf16[1,256,1024]{2,1,0:T(8,128)(2,1)}, u32[]{:S(2)}) copy-start(bf16[1,256,1024]{2,1,0:T(8,128)(2,1)} %get-tuple-element.174) | copy-start | bytes 1572868
where the time goes:
time: 152 us; the launch traced here: 151 us
  blocking collectives  46.5 us (31%)
  waiting for transfers between devices  39.3 us (26%)
  other arithmetic  28.5 us (19%)
  local copies, waits for them, and re-layouts  16.5 us (11%)
  between operations  10.8 us (7%)
  starting transfers between devices  7.6 us (5%)
  matrix products  1.79 us (1%)
    ppermute x1, waiting for transfers between devices, from_behind(): lax.ppermute(value, axis, [(source, source + steps) for source in range(f...  39.3 us
    all_gather x2, blocking collectives, entering(): everything = jax.tree.map(lambda part: lax.all_gather(part, axis), value)  37.9 us
    another operation x4, local copies, waits for them, and re-layouts, moments(): jnp.stack([jnp.sum(grad_y * grad_y), jnp.sum(grad_y * grad_x), jnp.sum(gr...  13 us
    psum x1, blocking collectives, per_device(): sums = lax.psum(placed, 'rows')  8.53 us
    concatenate x2, other arithmetic, per_device(): residual = jnp.concatenate(errors, axis=1).astype(jnp.bfloat16)  6.57 us
    reduce_sum x2, other arithmetic, moments(): jnp.sum(grad_x * error)  5.93 us
    mul x1, other arithmetic, moments(): grad_y = (window[2:, 1:-1] - window[:-2, 1:-1]) * 0.5  5.12 us
    ppermute x1, starting transfers between devices, from_behind(): lax.ppermute(value, axis, [(source, source + steps) for source in range(f...  5.01 us
  transfers between devices with their start and end apart: 3, of which 1 were waited for; matrix products, arithmetic and copies ran while one was open for 4% of the time, Pallas kernels for 0%

commit v1 on v0

v1 whole, which is shorter than its diff:
```python
import functools

import jax
import jax.numpy as jnp
import numpy as np
from jax import lax
from jax.experimental import pallas as pl
from jax.experimental.pallas import tpu as pltpu
from jax.sharding import PartitionSpec as P

PATCH = 1024
MAXOFF = 16
LAMBDA = 0.002
RIDGE = 0.05
EDGE = 32
SIDE = 128
BLOCK = 256
TILE = 64
MESH = pl.DeviceIdType.MESH


def invert_three(matrix):
    a, b, c = (matrix[0, 0], matrix[0, 1], matrix[0, 2])
    d, e, f = (matrix[1, 0], matrix[1, 1], matrix[1, 2])
    g, h, k = (matrix[2, 0], matrix[2, 1], matrix[2, 2])
    cof = np.array(
        [
            [e * k - f * h, c * h - b * k, b * f - c * e],
            [f * g - d * k, a * k - c * g, c * d - a * f],
            [d * h - e * g, b * g - a * h, a * e - b * d],
        ]
    )
    return cof / (a * (e * k - f * h) - b * (d * k - f * g) + c * (d * h - e * g))


def fit_table(pgy, pgx, patch, height, width):
    yy = ((np.arange(pgy) + 0.5) * patch - height / 2.0) / height
    xx = ((np.arange(pgx) + 0.5) * patch - width / 2.0) / width
    design = np.stack([np.repeat(yy, pgx), np.tile(xx, pgy), np.ones(pgy * pgx)], 1)
    ridge_matrix = np.array([[RIDGE, 0.0, 0.0], [0.0, RIDGE, 0.0], [0.0, 0.0, 0.0]])
    gram = design.T @ design + ridge_matrix
    return invert_three(gram) @ design.T


def register(G, R, pgy, pgx, table, peaks, sec, res_hbm, nodes, prev, cur, res, rmat, cmat, gmat, acc,
             sums, maps, cur_sem, res_sem, send_sem, recv_sem, rel_send, rel_recv,
             sum_send, sum_recv, map_send, map_recv):
    band, width = sec.shape[1], sec.shape[2]
    height = band * R
    blocks = width // BLOCK
    per_patch = PATCH // BLOCK
    g, r = lax.axis_index("gz"), lax.axis_index("rows")
    f32, bf16 = jnp.float32, jnp.bfloat16

    load = pltpu.make_async_copy(sec.at[0], cur, cur_sem)
    load.start()
    rows_all = band + 2 * EDGE
    prev[:, 0:SIDE] = jnp.zeros((rows_all, SIDE), bf16)
    prev[:, SIDE + width :] = jnp.zeros((rows_all, SIDE), bf16)

    @pl.when(r == 0)
    def _():
        prev[0:EDGE, :] = jnp.zeros((EDGE, width + 2 * SIDE), bf16)

    @pl.when(r == R - 1)
    def _():
        prev[EDGE + band :, :] = jnp.zeros((EDGE, width + 2 * SIDE), bf16)

    barrier = pltpu.get_barrier_semaphore()
    for d in range(1, R):
        pl.semaphore_signal(barrier, inc=1, device_id={"rows": lax.rem(r + d, R)}, device_id_type=MESH)
    for d in range(1, G):
        pl.semaphore_signal(barrier, inc=1, device_id={"gz": lax.rem(g + d, G)}, device_id_type=MESH)
    pl.semaphore_wait(barrier, R + G - 2)

    ahead = lax.rem(g + 1, G)

    def edge_copy(which):
        row = 0 if which == 0 else band - EDGE
        return pltpu.make_async_remote_copy(
            src_ref=sec.at[0, pl.ds(row, EDGE), :],
            dst_ref=prev.at[pl.ds(EDGE + row, EDGE), pl.ds(SIDE, width)],
            send_sem=send_sem.at[which], recv_sem=recv_sem.at[which],
            device_id={"gz": ahead}, device_id_type=MESH)

    def block_copy(c):
        col = pl.multiple_of(c * BLOCK, BLOCK)
        return pltpu.make_async_remote_copy(
            src_ref=sec.at[0, pl.ds(EDGE, band - 2 * EDGE), pl.ds(col, BLOCK)],
            dst_ref=prev.at[pl.ds(2 * EDGE, band - 2 * EDGE), pl.ds(SIDE + col, BLOCK)],
            send_sem=send_sem.at[2 + c], recv_sem=recv_sem.at[2 + c],
            device_id={"gz": ahead}, device_id_type=MESH)

    def relay_up():
        return pltpu.make_async_remote_copy(
            src_ref=prev.at[pl.ds(EDGE, EDGE), pl.ds(SIDE, width)],
            dst_ref=prev.at[pl.ds(EDGE + band, EDGE), pl.ds(SIDE, width)],
            send_sem=rel_send.at[0], recv_sem=rel_recv.at[0],
            device_id={"rows": lax.rem(r + R - 1, R)}, device_id_type=MESH)

    def relay_down():
        return pltpu.make_async_remote_copy(
            src_ref=prev.at[pl.ds(band, EDGE), pl.ds(SIDE, width)],
            dst_ref=prev.at[pl.ds(0, EDGE), pl.ds(SIDE, width)],
            send_sem=rel_send.at[1], recv_sem=rel_recv.at[1],
            device_id={"rows": lax.rem(r + 1, R)}, device_id_type=MESH)

    @pl.when(g < G - 1)
    def _():
        edge_copy(0).start()
        edge_copy(1).start()
        lax.fori_loop(0, blocks, lambda c, z: (block_copy(c).start(), z)[1], 0)

    @pl.when(g == 0)
    def _():
        def clear(t, z):
            prev[pl.ds(pl.multiple_of(t * EDGE, EDGE), EDGE), :] = jnp.zeros((EDGE, width + 2 * SIDE), bf16)
            return z

        lax.fori_loop(0, rows_all // EDGE, clear, 0)

    patch_row = r * band // PATCH
    rr = lax.broadcasted_iota(jnp.int32, (TILE, TILE + 2 * EDGE), 0)
    rk = lax.broadcasted_iota(jnp.int32, (TILE, TILE + 2 * EDGE), 1)
    ck = lax.broadcasted_iota(jnp.int32, (BLOCK + 2 * SIDE, BLOCK), 0)
    cn = lax.broadcasted_iota(jnp.int32, (BLOCK + 2 * SIDE, BLOCK), 1)
    rdiff = rk - rr - EDGE
    cdiff = ck - cn - SIDE
    for j in range(pgx):
        a = peaks[0, 0, patch_row, j]
        b = peaks[0, 1, patch_row, j]
        for n, step in enumerate((0, 1, -1)):
            rmat[j, n * TILE : (n + 1) * TILE, :] = jnp.where(rdiff == a + step, 1.0, 0.0).astype(bf16)
        cmat[j] = jnp.where(cdiff == b, 1.0, 0.0).astype(bf16)
        gmat[j] = jnp.where(cdiff == b + 1, 0.5, jnp.where(cdiff == b - 1, -0.5, 0.0)).astype(bf16)
    acc[...] = jnp.zeros_like(acc)
    load.wait()

    @pl.when(g > 0)
    def _():
        edge_copy(0).wait_recv()

        @pl.when(r > 0)
        def _():
            relay_up().start()

        edge_copy(1).wait_recv()

        @pl.when(r < R - 1)
        def _():
            relay_down().start()
            relay_up().wait_recv()

        @pl.when(r > 0)
        def _():
            relay_down().wait_recv()

        block_copy(0).wait_recv()

    tiles = band // TILE

    def fold(value):
        value = jnp.sum(value.reshape(value.shape[0] // 8, 8, BLOCK), axis=0)
        return sum(value[:, q : q + 128] for q in range(0, BLOCK, 128))

    def out_copy(c):
        col = pl.multiple_of(c * BLOCK, BLOCK)
        return pltpu.make_async_copy(res.at[:, pl.ds(col, BLOCK)], res_hbm.at[0, :, pl.ds(col, BLOCK)], res_sem.at[c])

    def body(c, z):
        @pl.when((g > 0) & (c + 1 < blocks))
        def _():
            block_copy(c + 1).wait_recv()

        j = c // per_patch
        col = pl.multiple_of(c * BLOCK, BLOCK)
        moved = []
        for t in range(tiles):
            window = prev[t * TILE : t * TILE + TILE + 2 * EDGE, pl.ds(col, BLOCK + 2 * SIDE)]
            moved.append(jnp.dot(rmat[j], window, preferred_element_type=f32).astype(bf16))
        parts = [jnp.concatenate([m[n * TILE : (n + 1) * TILE] for m in moved], axis=0) for n in range(3)]
        q = jnp.dot(parts[0], cmat[j], preferred_element_type=f32)
        lower = jnp.dot(parts[1], cmat[j], preferred_element_type=f32)
        upper = jnp.dot(parts[2], cmat[j], preferred_element_type=f32)
        gx = jnp.dot(parts[0], gmat[j], preferred_element_type=f32)
        gy = (lower - upper) * 0.5
        e = cur[:, pl.ds(col, BLOCK)].astype(f32) - q
        res[:, pl.ds(col, BLOCK)] = e.astype(bf16)
        out_copy(c).start()
        acc[j, 0] += fold(gy * gy)
        acc[j, 1] += fold(gy * gx)
        acc[j, 2] += fold(gx * gx)
        acc[j, 3] += fold(gy * e)
        acc[j, 4] += fold(gx * e)
        return z

    lax.fori_loop(0, blocks, body, 0)

    lane = lax.broadcasted_iota(jnp.int32, (8, 128), 1)
    row = lax.broadcasted_iota(jnp.int32, (8, 128), 0)
    mine = jnp.zeros((8, 128), f32)
    for j in range(pgx):
        for m in range(5):
            total = jnp.sum(jnp.sum(acc[j, m], axis=0, keepdims=True), axis=1, keepdims=True)
            mine = jnp.where((lane == patch_row * pgx + j) & (row == m), total, mine)
    sums[r] = mine

    def sum_copy(d, slot):
        return pltpu.make_async_remote_copy(
            src_ref=sums.at[slot], dst_ref=sums.at[slot], send_sem=sum_send.at[d], recv_sem=sum_recv.at[d],
            device_id={"rows": lax.rem(r + d, R)}, device_id_type=MESH)

    for d in range(1, R):
        sum_copy(d, r).start()
    peak_y = jnp.zeros((1, 128), f32)
    peak_x = jnp.zeros((1, 128), f32)
    for i in range(pgy):
        for j in range(pgx):
            here = lane[0:1] == i * pgx + j
            peak_y = jnp.where(here, peaks[0, 0, i, j].astype(f32), peak_y)
            peak_x = jnp.where(here, peaks[0, 1, i, j].astype(f32), peak_x)
    for d in range(1, R):
        sum_copy(d, lax.rem(r + R - d, R)).wait_recv()
    full = sums[0]
    for k in range(1, R):
        full = full + sums[k]

    damping = LAMBDA * PATCH * PATCH
    first = full[0:1] + damping
    cross = full[1:2]
    second = full[2:3] + damping
    det = first * second - cross * cross
    off_y = peak_y + (second * full[3:4] - cross * full[4:5]) / det
    off_x = peak_x + (first * full[4:5] - cross * full[3:4]) / det
    ty, tx = table[0:1], table[1:2]

    def lanes(value):
        return jnp.sum(value, axis=1, keepdims=True)

    pieces = [
        off_y,
        off_x,
        1.0 + lanes(off_y * ty) / height,
        lanes(off_y * tx) / width,
        lanes(off_x * ty) / height,
        1.0 + lanes(off_x * tx) / width,
    ]
    own = jnp.zeros((8, 128), f32)
    for k, piece in enumerate(pieces):
        own = jnp.where(row == k, jnp.broadcast_to(piece, (8, 128)), own)
    maps[g] = own

    def map_copy(d, slot):
        return pltpu.make_async_remote_copy(
            src_ref=maps.at[slot], dst_ref=maps.at[slot], send_sem=map_send.at[d], recv_sem=map_recv.at[d],
            device_id={"gz": lax.rem(g + d, G)}, device_id_type=MESH)

    for d in reversed(range(1, G)):
        @pl.when(g + d < G)
        def _():
            map_copy(d, g).start()

    for d in range(1, G):
        @pl.when(g - d >= 0)
        def _():
            map_copy(d, lax.rem(g + G - d, G)).wait_recv()

    def advance(s, u):
        uy, ux = u
        m = maps[s]
        return (m[2:3] * uy + m[3:4] * ux + m[0:1], m[4:5] * uy + m[5:6] * ux + m[1:2])

    zero = jnp.zeros((1, 128), f32)
    uy, ux = lax.fori_loop(0, g + 1, advance, (zero, zero))
    nodes[0:1] = uy
    nodes[1:2] = ux
    nodes[2:3] = off_y
    nodes[3:4] = off_x
    nodes[4:8] = jnp.zeros((4, 128), f32)

    lax.fori_loop(0, blocks, lambda c, z: (out_copy(c).wait(), z)[1], 0)

    @pl.when(g < G - 1)
    def _():
        edge_copy(0).wait_send()
        edge_copy(1).wait_send()
        lax.fori_loop(0, blocks, lambda c, z: (block_copy(c).wait_send(), z)[1], 0)

    @pl.when((g > 0) & (r > 0))
    def _():
        relay_up().wait_send()

    @pl.when((g > 0) & (r < R - 1))
    def _():
        relay_down().wait_send()

    for d in range(1, R):
        sum_copy(d, r).wait_send()
    for d in range(1, G):
        @pl.when(g + d < G)
        def _():
            map_copy(d, g).wait_send()


def spread_out(pgy, pgx, start_ref, nodes, res_in, field, offsets, res_out, buf, stage, in_sem, out_sem, field_sem):
    band, width = field.shape[2], field.shape[3]
    f32 = jnp.float32
    fetch = pltpu.make_async_copy(res_in, stage, in_sem)
    fetch.start()
    start = start_ref[0].astype(f32)
    cols = (lax.broadcasted_iota(jnp.int32, (1, width), 1).astype(f32) + 0.5) / PATCH - 0.5
    cols = jnp.clip(cols, 0.0, pgx - 1.0)
    weights = [jnp.maximum(0.0, 1.0 - jnp.abs(cols - j)) for j in range(pgx)]
    part = 64
    rows = lax.broadcasted_iota(jnp.int32, (part, 1), 0).astype(f32) + start
    put = pltpu.make_async_copy(stage, res_out, out_sem)
    copies = []
    for k in range(2):
        wide = []
        for i in range(pgy):
            line = jnp.zeros((1, width), f32)
            for j in range(pgx):
                p = i * pgx + j
                line = line + weights[j] * nodes[k : k + 1, p : p + 1]
            wide.append(line)
        for t in range(band // part):
            pos = jnp.clip((rows + (t * part + 0.5)) / PATCH - 0.5, 0.0, pgy - 1.0)
            block = jnp.zeros((part, width), f32)
            for i in range(pgy):
                block = block + jnp.maximum(0.0, 1.0 - jnp.abs(pos - i)) * wide[i]
            buf[k, t * part : (t + 1) * part, :] = block
            span = pl.ds(t * part, part)
            copy = pltpu.make_async_copy(buf.at[k, span, :], field.at[0, k, span, :], field_sem.at[len(copies)])
            copy.start()
            copies.append(copy)
        if k == 0:
            fetch.wait()
            put.start()
    offsets[...] = nodes[2:4, 0 : pgy * pgx]
    put.wait()
    for copy in copies:
        copy.wait()


def per_device(G, R, sections, peaks):
    band, width = sections.shape[1:]
    height = band * R
    pgy, pgx = height // PATCH, width // PATCH
    blocks = width // BLOCK
    f32, bf16 = jnp.float32, jnp.bfloat16
    table = np.zeros((8, 128), np.float32)
    table[:3, : pgy * pgx] = fit_table(pgy, pgx, PATCH, height, width)
    vmem = pl.BlockSpec(memory_space=pltpu.VMEM)
    smem = pl.BlockSpec(memory_space=pltpu.SMEM)
    anywhere = pl.BlockSpec(memory_space=pl.ANY)
    dma = pltpu.SemaphoreType.DMA
    residual, nodes = pl.pallas_call(
        functools.partial(register, G, R, pgy, pgx),
        name="register",
        out_shape=(jax.ShapeDtypeStruct((1, band, width), bf16), jax.ShapeDtypeStruct((8, 128), f32)),
        in_specs=[vmem, smem, anywhere],
        out_specs=(anywhere, vmem),
        scratch_shapes=[
            pltpu.VMEM((band + 2 * EDGE, width + 2 * SIDE), bf16),
            pltpu.VMEM((band, width), bf16),
            pltpu.VMEM((band, width), bf16),
            pltpu.VMEM((pgx, 3 * TILE, TILE + 2 * EDGE), bf16),
            pltpu.VMEM((pgx, BLOCK + 2 * SIDE, BLOCK), bf16),
            pltpu.VMEM((pgx, BLOCK + 2 * SIDE, BLOCK), bf16),
            pltpu.VMEM((pgx, 5, 8, 128), f32),
            pltpu.VMEM((R, 8, 128), f32),
            pltpu.VMEM((G, 8, 128), f32),
            dma, dma((blocks,)), dma((blocks + 2,)), dma((blocks + 2,)), dma((2,)), dma((2,)),
            dma((R,)), dma((R,)), dma((G,)), dma((G,)),
        ],
        compiler_params=pltpu.CompilerParams(collective_id=0, has_side_effects=True),
    )(jnp.asarray(table), peaks, sections)
    start = (lax.axis_index("rows") * band).astype(jnp.int32).reshape(1)
    field, offsets, residual = pl.pallas_call(
        functools.partial(spread_out, pgy, pgx),
        name="spread_out",
        out_shape=(
            jax.ShapeDtypeStruct((1, 2, band, width), f32),
            jax.ShapeDtypeStruct((2, pgy * pgx), f32),
            jax.ShapeDtypeStruct((1, band, width), bf16),
        ),
        in_specs=[smem, vmem, anywhere],
        out_specs=(anywhere, vmem, anywhere),
        scratch_shapes=[
            pltpu.VMEM((2, band, width), f32), pltpu.VMEM((1, band, width), bf16),
            dma, dma, dma((2 * (band // 64),)),
        ],
    )(start, nodes, residual)
    return field, offsets.reshape(1, 2, pgy, pgx), residual


def solution(mesh):
    return jax.shard_map(
        functools.partial(per_device, mesh.shape["gz"], mesh.shape["rows"]),
        mesh=mesh,
        in_specs=(P("gz", "rows", None), P("gz", None, None, None)),
        out_specs=(P("gz", None, "rows", None), P("gz", None, None, None), P("gz", "rows", None)),
        check_vma=False,
    )
```

time: 152 us -> 68.5 us (0.45)
  the two profiles are of different devices: /device:TPU:0 before, /device:TPU:8 now
where the time goes in v1:
time: 68.5 us; the launch traced here: 68.3 us
  Pallas kernels  67.6 us (99%)
    pallas_call x1, Pallas kernels, per_device(): pl.pallas_call(functools.partial(register, G, R, pgy, pgx), name='registe...  61.1 us
    pallas_call x1, Pallas kernels, per_device(): pl.pallas_call(functools.partial(spread_out, pgy, pgx), name='spread_out'...  6.59 us

profile of v1, /device:TPU:8, one launch (start us, length us, event | category | flops | bytes accessed | tf_op | source)
XLA Modules:
  0.0 68.3 jit_solution(11572483042560905256)
XLA Ops:
  0.6 61.1 %register.1 = (bf16[1,256,4096]{2,1,0:T(8,128)(2,1)}, f32[8,128]{1,0:T(8,128)}) custom-call(f32[8,128]{1,0:T(8,128)} %constant.8.clone.table, s32[1,2,1,4]{3,2,1,0:T(1,128)} %peaks.1, bf16[1,256,4096]{2,1,0:T(8,128)(2,1)} %sec.1), custom_call_target="tpu_custom_call" | custom-call | tf_op jit(solution)/shard_map/register/pallas_call | solution.py:357
  61.7 6.6 %spread_out.1 = (f32[1,2,256,4096]{3,2,1,0:T(8,128)}, f32[2,4]{1,0:T(2,128)}, bf16[1,256,4096]{2,1,0:T(8,128)(2,1)}) custom-call(s32[1]{0:T(128)} %bitcast.start_ref, f32[8,128]{1,0:T(8,128)} %get-tuple-element.8.nodes, bf16[1,256,4096]{2,1,0:T(8,128)(2,1)} %get-tuple-element.9.res_in), custom_call_target="tpu_custom_call" | custom-call | tf_op jit(solution)/shard_map/spread_out/pallas_call | solution.py:379

commit v2 on v1

--- a/solution.py
+++ b/solution.py
@@ -42,8 +42,8 @@
     return invert_three(gram) @ design.T
 
 
-def register(G, R, pgy, pgx, table, peaks, sec, res_hbm, nodes, prev, cur, res, rmat, cmat, gmat, acc,
-             sums, maps, cur_sem, res_sem, send_sem, recv_sem, rel_send, rel_recv,
+def register(G, R, pgy, pgx, table, peaks_hbm, sec, res_hbm, nodes, prev, cur, res, rmat, cmat, gmat, acc,
+             sums, maps, peaks, peak_sem, cur_sem, res_sem, send_sem, recv_sem, rel_send, rel_recv,
              sum_send, sum_recv, map_send, map_recv):
     band, width = sec.shape[1], sec.shape[2]
     height = band * R
@@ -52,6 +52,13 @@
     g, r = lax.axis_index("gz"), lax.axis_index("rows")
     f32, bf16 = jnp.float32, jnp.bfloat16
 
+    barrier = pltpu.get_barrier_semaphore()
+    for d in range(1, R):
+        pl.semaphore_signal(barrier, inc=1, device_id={"rows": lax.rem(r + d, R)}, device_id_type=MESH)
+    for d in range(1, G):
+        pl.semaphore_signal(barrier, inc=1, device_id={"gz": lax.rem(g + d, G)}, device_id_type=MESH)
+    peak_load = pltpu.make_async_copy(peaks_hbm, peaks, peak_sem)
+    peak_load.start()
     load = pltpu.make_async_copy(sec.at[0], cur, cur_sem)
     load.start()
     rows_all = band + 2 * EDGE
@@ -66,11 +73,6 @@
     def _():
         prev[EDGE + band :, :] = jnp.zeros((EDGE, width + 2 * SIDE), bf16)
 
-    barrier = pltpu.get_barrier_semaphore()
-    for d in range(1, R):
-        pl.semaphore_signal(barrier, inc=1, device_id={"rows": lax.rem(r + d, R)}, device_id_type=MESH)
-    for d in range(1, G):
-        pl.semaphore_signal(barrier, inc=1, device_id={"gz": lax.rem(g + d, G)}, device_id_type=MESH)
     pl.semaphore_wait(barrier, R + G - 2)
 
     ahead = lax.rem(g + 1, G)
@@ -83,13 +85,21 @@
             send_sem=send_sem.at[which], recv_sem=recv_sem.at[which],
             device_id={"gz": ahead}, device_id_type=MESH)
 
-    def block_copy(c):
-        col = pl.multiple_of(c * BLOCK, BLOCK)
-        return pltpu.make_async_remote_copy(
-            src_ref=sec.at[0, pl.ds(EDGE, band - 2 * EDGE), pl.ds(col, BLOCK)],
-            dst_ref=prev.at[pl.ds(2 * EDGE, band - 2 * EDGE), pl.ds(SIDE + col, BLOCK)],
-            send_sem=send_sem.at[2 + c], recv_sem=recv_sem.at[2 + c],
+    def span_copy(k, col, count):
+        return pltpu.make_async_remote_copy(
+            src_ref=sec.at[0, pl.ds(EDGE, band - 2 * EDGE), pl.ds(col, count)],
+            dst_ref=prev.at[pl.ds(2 * EDGE, band - 2 * EDGE), pl.ds(SIDE + col, count)],
+            send_sem=send_sem.at[2 + k], recv_sem=recv_sem.at[2 + k],
             device_id={"gz": ahead}, device_id_type=MESH)
+
+    def head_copy():
+        return span_copy(0, 0, BLOCK + SIDE)
+
+    def middle_copy(k):
+        return span_copy(k, pl.multiple_of(k * BLOCK + SIDE, SIDE), BLOCK)
+
+    def tail_copy():
+        return span_copy(blocks - 1, width - BLOCK + SIDE, BLOCK - SIDE)
 
     def relay_up():
         return pltpu.make_async_remote_copy(
@@ -109,7 +119,9 @@
     def _():
         edge_copy(0).start()
         edge_copy(1).start()
-        lax.fori_loop(0, blocks, lambda c, z: (block_copy(c).start(), z)[1], 0)
+        head_copy().start()
+        lax.fori_loop(1, blocks - 1, lambda k, z: (middle_copy(k).start(), z)[1], 0)
+        tail_copy().start()
 
     @pl.when(g == 0)
     def _():
@@ -120,6 +132,7 @@
         lax.fori_loop(0, rows_all // EDGE, clear, 0)
 
     patch_row = r * band // PATCH
+    peak_load.wait()
     rr = lax.broadcasted_iota(jnp.int32, (TILE, TILE + 2 * EDGE), 0)
     rk = lax.broadcasted_iota(jnp.int32, (TILE, TILE + 2 * EDGE), 1)
     ck = lax.broadcasted_iota(jnp.int32, (BLOCK + 2 * SIDE, BLOCK), 0)
@@ -155,7 +168,7 @@
         def _():
             relay_down().wait_recv()
 
-        block_copy(0).wait_recv()
+        head_copy().wait_recv()
 
     tiles = band // TILE
 
@@ -168,9 +181,13 @@
         return pltpu.make_async_copy(res.at[:, pl.ds(col, BLOCK)], res_hbm.at[0, :, pl.ds(col, BLOCK)], res_sem.at[c])
 
     def body(c, z):
-        @pl.when((g > 0) & (c + 1 < blocks))
-        def _():
-            block_copy(c + 1).wait_recv()
+        @pl.when((g > 0) & (c > 0) & (c < blocks - 1))
+        def _():
+            middle_copy(c).wait_recv()
+
+        @pl.when((g > 0) & (c == blocks - 1))
+        def _():
+            tail_copy().wait_recv()
 
         j = c // per_patch
         col = pl.multiple_of(c * BLOCK, BLOCK)
@@ -232,7 +249,11 @@
     det = first * second - cross * cross
     off_y = peak_y + (second * full[3:4] - cross * full[4:5]) / det
     off_x = peak_x + (first * full[4:5] - cross * full[3:4]) / det
-    ty, tx = table[0:1], table[1:2]
+    ty = jnp.zeros((1, 128), f32)
+    tx = jnp.zeros((1, 128), f32)
+    for p in range(pgy * pgx):
+        ty = jnp.where(lane[0:1] == p, float(table[0, p]), ty)
+        tx = jnp.where(lane[0:1] == p, float(table[1, p]), tx)
 
     def lanes(value):
         return jnp.sum(value, axis=1, keepdims=True)
@@ -260,6 +281,26 @@
         def _():
             map_copy(d, g).start()
 
+    lax.fori_loop(0, blocks, lambda c, z: (out_copy(c).wait(), z)[1], 0)
+
+    @pl.when(g < G - 1)
+    def _():
+        edge_copy(0).wait_send()
+        edge_copy(1).wait_send()
+        head_copy().wait_send()
+        lax.fori_loop(1, blocks - 1, lambda k, z: (middle_copy(k).wait_send(), z)[1], 0)
+        tail_copy().wait_send()
+
+    @pl.when((g > 0) & (r > 0))
+    def _():
+        relay_up().wait_send()
+
+    @pl.when((g > 0) & (r < R - 1))
+    def _():
+        relay_down().wait_send()
+
+    for d in range(1, R):
+        sum_copy(d, r).wait_send()
     for d in range(1, G):
         @pl.when(g - d >= 0)
         def _():
@@ -278,24 +319,6 @@
     nodes[3:4] = off_x
     nodes[4:8] = jnp.zeros((4, 128), f32)
 
-    lax.fori_loop(0, blocks, lambda c, z: (out_copy(c).wait(), z)[1], 0)
-
-    @pl.when(g < G - 1)
-    def _():
-        edge_copy(0).wait_send()
-        edge_copy(1).wait_send()
-        lax.fori_loop(0, blocks, lambda c, z: (block_copy(c).wait_send(), z)[1], 0)
-
-    @pl.when((g > 0) & (r > 0))
-    def _():
-        relay_up().wait_send()
-
-    @pl.when((g > 0) & (r < R - 1))
-    def _():
-        relay_down().wait_send()
-
-    for d in range(1, R):
-        sum_copy(d, r).wait_send()
     for d in range(1, G):
         @pl.when(g + d < G)
         def _():
@@ -307,30 +330,33 @@
     f32 = jnp.float32
     fetch = pltpu.make_async_copy(res_in, stage, in_sem)
     fetch.start()
-    start = start_ref[0].astype(f32)
-    cols = (lax.broadcasted_iota(jnp.int32, (1, width), 1).astype(f32) + 0.5) / PATCH - 0.5
+    cols = (lax.broadcasted_iota(jnp.int32, (8, width), 1).astype(f32) + 0.5) / PATCH - 0.5
     cols = jnp.clip(cols, 0.0, pgx - 1.0)
     weights = [jnp.maximum(0.0, 1.0 - jnp.abs(cols - j)) for j in range(pgx)]
-    part = 64
-    rows = lax.broadcasted_iota(jnp.int32, (part, 1), 0).astype(f32) + start
+    part = 32
     put = pltpu.make_async_copy(stage, res_out, out_sem)
     copies = []
     for k in range(2):
         wide = []
         for i in range(pgy):
-            line = jnp.zeros((1, width), f32)
+            line = jnp.zeros((8, width), f32)
             for j in range(pgx):
                 p = i * pgx + j
                 line = line + weights[j] * nodes[k : k + 1, p : p + 1]
             wide.append(line)
         for t in range(band // part):
-            pos = jnp.clip((rows + (t * part + 0.5)) / PATCH - 0.5, 0.0, pgy - 1.0)
-            block = jnp.zeros((part, width), f32)
-            for i in range(pgy):
-                block = block + jnp.maximum(0.0, 1.0 - jnp.abs(pos - i)) * wide[i]
-            buf[k, t * part : (t + 1) * part, :] = block
-            span = pl.ds(t * part, part)
-            copy = pltpu.make_async_copy(buf.at[k, span, :], field.at[0, k, span, :], field_sem.at[len(copies)])
+            slot = 0 if pgy == 1 else t
+            for q in range(0, part, 8) if pgy > 1 or t == 0 else ():
+                if pgy == 1:
+                    block = wide[0]
+                else:
+                    rows = lax.broadcasted_iota(jnp.int32, (8, 1), 0).astype(f32) + start_ref[0].astype(f32)
+                    pos = jnp.clip((rows + (t * part + q + 0.5)) / PATCH - 0.5, 0.0, pgy - 1.0)
+                    block = sum(jnp.maximum(0.0, 1.0 - jnp.abs(pos - i)) * wide[i] for i in range(pgy))
+                buf[k, slot * part + q : slot * part + q + 8, :] = block
+            copy = pltpu.make_async_copy(
+                buf.at[k, pl.ds(slot * part, part), :], field.at[0, k, pl.ds(t * part, part), :],
+                field_sem.at[len(copies)])
             copy.start()
             copies.append(copy)
         if k == 0:
@@ -348,17 +374,16 @@
     pgy, pgx = height // PATCH, width // PATCH
     blocks = width // BLOCK
     f32, bf16 = jnp.float32, jnp.bfloat16
-    table = np.zeros((8, 128), np.float32)
-    table[:3, : pgy * pgx] = fit_table(pgy, pgx, PATCH, height, width)
+    table = fit_table(pgy, pgx, PATCH, height, width).astype(np.float32)
     vmem = pl.BlockSpec(memory_space=pltpu.VMEM)
     smem = pl.BlockSpec(memory_space=pltpu.SMEM)
     anywhere = pl.BlockSpec(memory_space=pl.ANY)
     dma = pltpu.SemaphoreType.DMA
     residual, nodes = pl.pallas_call(
-        functools.partial(register, G, R, pgy, pgx),
+        functools.partial(register, G, R, pgy, pgx, table),
         name="register",
         out_shape=(jax.ShapeDtypeStruct((1, band, width), bf16), jax.ShapeDtypeStruct((8, 128), f32)),
-        in_specs=[vmem, smem, anywhere],
+        in_specs=[anywhere, anywhere],
         out_specs=(anywhere, vmem),
         scratch_shapes=[
             pltpu.VMEM((band + 2 * EDGE, width + 2 * SIDE), bf16),
@@ -370,11 +395,12 @@
             pltpu.VMEM((pgx, 5, 8, 128), f32),
             pltpu.VMEM((R, 8, 128), f32),
             pltpu.VMEM((G, 8, 128), f32),
-            dma, dma((blocks,)), dma((blocks + 2,)), dma((blocks + 2,)), dma((2,)), dma((2,)),
+            pltpu.SMEM((1, 2, pgy, pgx), jnp.int32),
+            dma, dma, dma((blocks,)), dma((blocks + 2,)), dma((blocks + 2,)), dma((2,)), dma((2,)),
             dma((R,)), dma((R,)), dma((G,)), dma((G,)),
         ],
         compiler_params=pltpu.CompilerParams(collective_id=0, has_side_effects=True),
-    )(jnp.asarray(table), peaks, sections)
+    )(peaks, sections)
     start = (lax.axis_index("rows") * band).astype(jnp.int32).reshape(1)
     field, offsets, residual = pl.pallas_call(
         functools.partial(spread_out, pgy, pgx),
@@ -387,8 +413,8 @@
         in_specs=[smem, vmem, anywhere],
         out_specs=(anywhere, vmem, anywhere),
         scratch_shapes=[
-            pltpu.VMEM((2, band, width), f32), pltpu.VMEM((1, band, width), bf16),
-            dma, dma, dma((2 * (band // 64),)),
+            pltpu.VMEM((2, 32 if pgy == 1 else band, width), f32), pltpu.VMEM((1, band, width), bf16),
+            dma, dma, dma((2 * (band // 32),)),
         ],
     )(start, nodes, residual)
     return field, offsets.reshape(1, 2, pgy, pgx), residual

time: 68.5 us -> 67 us (0.978)
  Pallas kernels: 67.6 us -> 66.2 us
    pallas_call x1, Pallas kernels: 61.1 us -> 59.5 us  [per_device(): pl.pallas_call(functools.partial(register, G, R, pgy, pgx, table), name='...]
where the time goes in v2:
time: 67 us; the launch traced here: 66.8 us
  Pallas kernels  66.2 us (99%)
    pallas_call x1, Pallas kernels, per_device(): pl.pallas_call(functools.partial(register, G, R, pgy, pgx, table), name='...  59.5 us
    pallas_call x1, Pallas kernels, per_device(): pl.pallas_call(functools.partial(spread_out, pgy, pgx), name='spread_out'...  6.71 us

profile of v2, /device:TPU:8, one launch (start us, length us, event | category | flops | bytes accessed | tf_op | source)
XLA Modules:
  0.0 66.8 jit_solution(1073576123501033459)
XLA Ops:
  0.6 59.5 %register.1 = (bf16[1,256,4096]{2,1,0:T(8,128)(2,1)}, f32[8,128]{1,0:T(8,128)}) custom-call(s32[1,2,1,4]{3,2,1,0:T(1,128)} %peaks_hbm.1, bf16[1,256,4096]{2,1,0:T(8,128)(2,1)} %sec.1), custom_call_target="tpu_custom_call" | custom-call | tf_op jit(solution)/shard_map/register/pallas_call | solution.py:382
  60.1 6.7 %spread_out.1 = (f32[1,2,256,4096]{3,2,1,0:T(8,128)}, f32[2,4]{1,0:T(2,128)}, bf16[1,256,4096]{2,1,0:T(8,128)(2,1)}) custom-call(s32[1]{0:T(128)} %bitcast.start_ref, f32[8,128]{1,0:T(8,128)} %get-tuple-element.8.nodes, bf16[1,256,4096]{2,1,0:T(8,128)(2,1)} %get-tuple-element.9.res_in), custom_call_target="tpu_custom_call" | custom-call | tf_op jit(solution)/shard_map/spread_out/pallas_call | solution.py:405
